TPU v7x, 256 devices: a whole 4x4x8 slice. The times are simulated.
256 devices in a mesh: section: 8 (over z_lo, x), dp: 32 (over z_hi, y, core).
Axes of the slice: x: 4, y: 4, z: 8 (z_hi: 4, z_lo: 2; z = z_hi * 2 + z_lo), core: 2. Of those that a mesh axis runs over, the one named last changes fastest.
Arguments:
- ln_input: bfloat16 [8, 4096, 12288], P('section', 'dp'), may hold values from -6 to 6
- ln_grad: bfloat16 [8, 4096, 12288], P('section', 'dp'), may hold values from -6 to 6
- top_grad: bfloat16 [8, 4096, 12288], P('section', 'dp'), may hold values from -6 to 6
- ln_gain: float32 [8, 12288], P('section'), may hold values from 0.1 to 1.9
- hidden: bfloat16 [8, 4096, 64], P('section', 'dp'), may hold values from -8 to 8
- master: float32 [8, 64, 12288], P('section', 'dp'), may hold values from -6 to 6
- moment: float32 [8, 64, 12288], P('section', 'dp'), may hold values from -6 to 6
- second: float32 [8, 64, 12288], P('section', 'dp'), may hold values from 0.1 to 4
Outputs:
- new_master: float32 [8, 64, 12288], P('section', 'dp')
- new_moment: float32 [8, 64, 12288], P('section', 'dp')
- new_second: float32 [8, 64, 12288], P('section', 'dp')
- weights: bfloat16 [8, 64, 12288], P('section')
All inputs are finite; a program needn't handle non-finite values.
Results may differ from a plain program's by a relative error of at most 0.0078.
Values may be sent and summed in bfloat16 or wider, within the bound.
A program may use at most 64 MiB of HBM per device.

v0:
```python
import jax
import jax.numpy as jnp
from jax import lax
from jax.sharding import Mesh
from jax.sharding import PartitionSpec as P

STEP = 20
DP = ("dp_0", "dp_1", "dp_2")


def shifted_2(value, axis, steps):
    count = lax.axis_size(axis)
    first, last = (max(0, -steps), min(count, count - steps))
    return lax.ppermute(value, axis, [(source, source + steps) for source in range(first, last)])


def split_up(x, dim, devices):
    before, after = (x.shape[:dim], x.shape[dim + 1 :])
    return jnp.moveaxis(x.reshape(*before, devices, -1, *after), dim, 0)


def sent_and_summed(x, axis, dim):
    devices = lax.axis_size(axis)
    blocks = lax.all_to_all(split_up(x, dim, devices), axis, 0, 0, tiled=True)
    return jnp.sum(blocks.astype(jnp.float32), axis=0)


def summed_rows(x, axes, dim):
    far, near = axes
    own = sent_and_summed(split_up(x, dim, lax.axis_size(far)), near, dim + 1)
    return jnp.sum(
        lax.all_to_all(own.astype(jnp.bfloat16), far, 0, 0, tiled=True).astype(jnp.float32), axis=0
    )


def from_everyone(x, axis):
    copies = jnp.broadcast_to(x, (lax.axis_size(axis), *x.shape))
    return lax.all_to_all(copies, axis, split_axis=0, concat_axis=0, tiled=True)


def in_order(blocks, dim):
    blocks = jnp.moveaxis(blocks, 0, dim)
    shape = blocks.shape
    return blocks.reshape(*shape[:dim], shape[dim] * shape[dim + 1], *shape[dim + 2 :])


def gather_axes(x, axes, dim):
    far, near = axes
    first = from_everyone(x, far)
    blocks = jnp.swapaxes(from_everyone(first, near), 0, 1)
    return in_order(blocks.reshape(-1, *x.shape), dim)


def layer_back(ln_input, ln_grad, top_grad, ln_gain):
    values = ln_input.astype(jnp.float32)
    row_mean = jnp.mean(values, axis=-1, keepdims=True)
    centred = values - row_mean
    inv_std = 1.0 / jnp.sqrt(jnp.mean(centred * centred, axis=-1, keepdims=True) + 1e-05)
    normed = centred * inv_std
    scaled = ln_grad.astype(jnp.float32) * ln_gain[:, None, :]
    inner = (
        scaled
        - jnp.mean(scaled, axis=-1, keepdims=True)
        - normed * jnp.mean(scaled * normed, axis=-1, keepdims=True)
    )
    return (top_grad.astype(jnp.float32) + inner * inv_std).astype(jnp.bfloat16)


def adam_update(grad, master, moment, second):
    new_moment = 0.9 * moment + 0.1 * grad
    new_second = 0.95 * second + 0.05 * grad * grad
    first_fix = 1.0 - 0.9**STEP
    second_fix = 1.0 - 0.95**STEP
    update = new_moment / first_fix / (jnp.sqrt(new_second / second_fix) + 1e-08)
    new_master = master - 0.05 * (update + 0.1 * master)
    return (new_master, new_moment, new_second)


def term_maker(columns, received):
    return lax.dot_general(
        columns, received, (((0,), (0,)), ((), ())), preferred_element_type=jnp.float32
    )


def owner_columns(columns, group_size, row_dev, first, last_row):
    tokens_here = columns.shape[0]
    grouped = columns.reshape(tokens_here, group_size, row_dev)
    return grouped.reshape(tokens_here, group_size * (last_row - first))


def shards(ln_input, ln_grad, top_grad, ln_gain, hidden, master, moment, second):
    passed = layer_back(ln_input, ln_grad, top_grad, ln_gain)
    is_last = lax.axis_index("section") == lax.axis_size("section") - 1
    row_dev = master.shape[1]
    width = master.shape[2]
    group_size = lax.axis_size(DP)
    own_cols = hidden[0]
    shifted = shifted_2(passed, "section", -1)
    received = jnp.where(is_last, top_grad, shifted)[0]
    bounds = (0, row_dev)
    first, last_row = bounds
    count = last_row - first
    cols = owner_columns(own_cols, group_size, row_dev, first, last_row)
    grad = summed_rows(
        term_maker(cols, received).astype(jnp.bfloat16), (("dp_0", "dp_1"), "dp_2"), 0
    )
    state = adam_update(
        grad, master[0, first:last_row], moment[0, first:last_row], second[0, first:last_row]
    )
    masters = state[0]
    moments = state[1]
    seconds = state[2]
    pieces = gather_axes(state[0].astype(jnp.bfloat16), (("dp_0", "dp_1"), "dp_2"), 0)
    gathered = pieces.reshape(group_size, count, width)
    weights = gathered.reshape(group_size * row_dev, width)
    return (masters[None], moments[None], seconds[None], weights[None])


def solution(mesh):
    finer = Mesh(
        mesh.devices.reshape(mesh.shape["section"], 4, 4, 2), ("section", "dp_0", "dp_1", "dp_2")
    )
    return jax.shard_map(
        shards,
        mesh=finer,
        in_specs=(
            P("section", DP, None),
            P("section", DP, None),
            P("section", DP, None),
            P("section", None),
            P("section", DP, None),
            P("section", DP, None),
            P("section", DP, None),
            P("section", DP, None),
        ),
        out_specs=(
            P("section", DP, None),
            P("section", DP, None),
            P("section", DP, None),
            P("section", None, None),
        ),
        check_vma=False,
    )
```

profile of v0, /device:TPU:3, one launch (start us, length us, event | category | flops | bytes accessed | tf_op | source)
XLA Modules:
  0.0 175.1 jit_solution(5630410384963327978)
XLA Ops:
  0.6 0.0 copy-start
  0.6 0.0 copy-start.1
  0.7 0.0 copy-start.2
  0.7 2.5 %convert_reduce_fusion = f32[128]{0:T(128)S(1)} fusion(bf16[1,128,12288]{2,1,0:T(8,128)(2,1)} %param.8), kind=kLoop, calls=%fused_computation.3 | loop fusion | flops 3145600 | bytes 3146240 | tf_op jit(solution)/shard_map/reduce_sum | solution.py:56
  3.2 0.3 copy-done.1
  3.5 1.0 fusion.10
  4.5 0.0 copy-done.2
  4.5 0.0 copy-start.3
  4.5 0.0 copy-start.7
  4.5 3.1 %fusion.11 = (f32[128]{0:T(128)S(1)}, f32[128]{0:T(128)S(1)}) fusion(bf16[1,128,12288]{2,1,0:T(8,128)(2,1)S(1)} %copy-done.2, f32[12288]{0:T(1024)} %bitcast.47, f32[128]{0:T(128)S(1)} %add_rsqrt_fusion, f32[128]{0:T(128)S(1)} %broadcast_multiply_fusion.1, bf16[1,128,12288]{2,1,0:T(8,128)(2,1)S(1)} %copy-done.1), kind=kLoop, calls=%fused_computation.15 | loop fusion | flops 12582656 | bytes 6342656 | tf_op jit(solution)/shard_map/reduce_sum | solution.py:63
  7.6 0.0 copy-done.3
  7.7 0.0 copy-done.7
  7.7 3.7 %fusion.9 = bf16[1,128,12288]{2,1,0:T(8,128)(2,1)} fusion(bf16[1,128,12288]{2,1,0:T(8,128)(2,1)S(1)} %copy-done.1, bf16[1,128,12288]{2,1,0:T(8,128)(2,1)S(1)} %copy-done.2, bf16[1,128,12288]{2,1,0:T(8,128)(2,1)S(1)} %copy-done.3, f32[128]{0:T(128)S(1)} %get-tuple-element.9, f32[128]{0:T(128)S(1)} %add_rsqrt_fusion, f32[128]{0:T(128)S(1)} %broadcast_multiply_fusion.1, ...), kind=kLoop, calls=%fused_computation.12 | loop fusion | flops 18874368 | bytes 12634112 | tf_op jit(solution)/shard_map/convert_element_type | solution.py:66
  11.4 1.9 %collective-permute-start = (bf16[1,128,12288]{2,1,0:T(8,128)(2,1)}, bf16[1,128,12288]{2,1,0:T(8,128)(2,1)}, u32[]{:S(2)}, u32[]{:S(2)}) collective-permute-start(bf16[1,128,12288]{2,1,0:T(8,128)(2,1)} %fusion.9), channel_id=1, source_target_pairs={{32,0},{64,32},{96,64},{128,96},{160,128},{192,160},{224,192},{33,... | collective-permute-start | bytes 9437192 | tf_op jit(solution)/shard_map/ppermute | solution.py:14
  13.3 69.3 %collective-permute-done = bf16[1,128,12288]{2,1,0:T(8,128)(2,1)} collective-permute-done((bf16[1,128,12288]{2,1,0:T(8,128)(2,1)}, bf16[1,128,12288]{2,1,0:T(8,128)(2,1)}, u32[]{:S(2)}, u32[]{:S(2)}) %collective-permute-start) | collective-permute-done | bytes 3145760 | tf_op jit(solution)/shard_map/ppermute | solution.py:14
  82.5 0.0 copy-done
  82.5 3.8 %fusion = bf16[64,12288]{1,0:T(8,128)(2,1)} fusion(bf16[1,128,12288]{2,1,0:T(8,128)(2,1)S(1)} %copy-done.3, bf16[1,128,12288]{2,1,0:T(8,128)(2,1)} %collective-permute-done, pred[]{:T(512)S(6)} %eq.3, bf16[1,128,64]{1,2,0:T(8,128)(2,1)S(1)} %copy-done), kind=kOutput, calls=%fused_computation.1 | convolution fusion | flops 203685888 | bytes 7880705 | tf_op jit(solution)/shard_map/dot_general | solution.py:80
  86.4 3.4 %reshape_reshape.3 = bf16[16,2,2,12288]{3,2,1,0:T(2,128)(2,1)S(1)} reshape(bf16[64,12288]{1,0:T(8,128)(2,1)} %fusion) | data formatting | bytes 3145728 | tf_op jit(solution)/shard_map/reshape;reshape | solution.py:19
  89.8 1.3 copy.25
  91.1 6.2 %all_to_all.20 = bf16[2,16,2,12288]{3,2,1,0:T(2,128)(2,1)S(1)} all-to-all(bf16[2,16,2,12288]{3,2,1,0:T(2,128)(2,1)S(1)} %bitcast.45), channel_id=1, replica_groups=mesh['section'=8,'dp_0'=4,'dp_1'=4,'dp_2'=2] {'dp_2'}, dimensions={0} | all-to-all | bytes 3145728 | tf_op jit(solution)/shard_map/all_to_all | solution.py:24
  97.3 0.0 copy-start.4
  97.3 0.0 copy-start.5
  97.3 0.0 copy-start.6
  97.3 3.3 %reduce_sum.63 = bf16[16,2,12288]{2,1,0:T(2,128)(2,1)S(1)} reduce(bf16[2,16,2,12288]{3,2,1,0:T(2,128)(2,1)S(1)} %all_to_all.20, bf16[]{:T(256)} %constant.30.clone.1), dimensions={0}, to_apply=%region_4.5 | reduce | flops 393216 | bytes 2359298 | tf_op jit(solution)/shard_map/reduce_sum | solution.py:25
  100.6 31.5 %all_to_all.21 = bf16[16,2,12288]{2,1,0:T(2,128)(2,1)S(1)} all-to-all(bf16[16,2,12288]{2,1,0:T(2,128)(2,1)S(1)} %reduce_sum.63), channel_id=1, replica_groups=mesh['section'=8,'dp_0'=4,'dp_1'=4,'dp_2'=2] {'dp_0','dp_1'}, dimensions={0} | all-to-all | bytes 1572864 | tf_op jit(solution)/shard_map/all_to_all | solution.py:32
  132.1 0.7 convert_reduce_fusion.1
  132.8 0.0 copy-done.4
  132.8 0.0 copy-done.5
  132.8 0.0 copy-done.6
  132.8 0.3 fusion.24
  133.1 1.5 broadcast_in_dim.4
  134.6 6.9 %all-to-all-start.2 = ((bf16[16,2,12288]{2,1,0:T(2,128)(2,1)}), bf16[16,2,12288]{2,1,0:T(2,128)(2,1)S(1)}, u32[]{:S(2)}, u32[]{:S(2)}) async-start(bf16[16,2,12288]{2,1,0:T(2,128)(2,1)} %broadcast_in_dim.4), calls=%async_computation.2 | async-start | bytes 1572864 | tf_op jit(solution)/shard_map/all_to_all | solution.py:38
  141.5 1.0 multiply_subtract_fusion
  142.5 21.4 %all-to-all-done.2 = bf16[16,2,12288]{2,1,0:T(2,128)(2,1)S(1)} async-done(((bf16[16,2,12288]{2,1,0:T(2,128)(2,1)}), bf16[16,2,12288]{2,1,0:T(2,128)(2,1)S(1)}, u32[]{:S(2)}, u32[]{:S(2)}) %all-to-all-start.2) | async-done | bytes 786464 | tf_op jit(solution)/shard_map/all_to_all | solution.py:38
  164.0 1.4 broadcast_in_dim.5
  165.4 6.7 %all_to_all.22 = bf16[2,16,2,12288]{3,2,1,0:T(2,128)(2,1)S(1)} all-to-all(bf16[2,16,2,12288]{3,2,1,0:T(2,128)(2,1)S(1)} %broadcast_in_dim.5), channel_id=1, replica_groups=mesh['section'=8,'dp_0'=4,'dp_1'=4,'dp_2'=2] {'dp_2'}, dimensions={0} | all-to-all | bytes 3145728 | tf_op jit(solution)/shard_map/all_to_all | solution.py:38
  172.1 1.4 copy.22
  173.5 1.5 broadcast_in_dim_reshape_reshape_reshape_reshape.3
  (3 shorter events, 0.0 us)
Async XLA Ops:
  0.6 81.9 %copy-start = (bf16[1,128,64]{1,2,0:T(8,128)(2,1)S(1)}, bf16[1,128,64]{1,2,0:T(8,128)(2,1)}, u32[]{:S(2)}) copy-start(bf16[1,128,64]{1,2,0:T(8,128)(2,1)} %param.12) | copy-start | bytes 49156
  0.6 2.8 %copy-start.1 = (bf16[1,128,12288]{2,1,0:T(8,128)(2,1)S(1)}, bf16[1,128,12288]{2,1,0:T(8,128)(2,1)}, u32[]{:S(2)}) copy-start(bf16[1,128,12288]{2,1,0:T(8,128)(2,1)} %param.8) | copy-start | bytes 9437188
  0.7 3.9 %copy-start.2 = (bf16[1,128,12288]{2,1,0:T(8,128)(2,1)S(1)}, bf16[1,128,12288]{2,1,0:T(8,128)(2,1)}, u32[]{:S(2)}) copy-start(bf16[1,128,12288]{2,1,0:T(8,128)(2,1)} %param.9) | copy-start | bytes 9437188
  4.5 3.1 %copy-start.3 = (bf16[1,128,12288]{2,1,0:T(8,128)(2,1)S(1)}, bf16[1,128,12288]{2,1,0:T(8,128)(2,1)}, u32[]{:S(2)}) copy-start(bf16[1,128,12288]{2,1,0:T(8,128)(2,1)} %param.10) | copy-start | bytes 9437188
  4.5 3.1 %copy-start.7 = (f32[1,12288]{1,0:T(1,128)S(1)}, f32[1,12288]{1,0:T(1,128)}, u32[]{:S(2)}) copy-start(f32[1,12288]{1,0:T(1,128)} %param.11) | copy-start | bytes 147460
  11.4 71.2 %collective-permute-start = (bf16[1,128,12288]{2,1,0:T(8,128)(2,1)}, bf16[1,128,12288]{2,1,0:T(8,128)(2,1)}, u32[]{:S(2)}, u32[]{:S(2)}) collective-permute-start(bf16[1,128,12288]{2,1,0:T(8,128)(2,1)} %fusion.9), channel_id=1, source_target_pairs={{32,0},{64,32},{96,64},{128,96},{160,128},{192,160},{224,192},{33,... | collective-permute-start | bytes 9437192 | tf_op jit(solution)/shard_map/ppermute | solution.py:14
  97.3 35.5 %copy-start.4 = (f32[1,2,12288]{2,1,0:T(2,128)S(1)}, f32[1,2,12288]{2,1,0:T(2,128)}, u32[]{:S(2)}) copy-start(f32[1,2,12288]{2,1,0:T(2,128)} %param.13) | copy-start | bytes 294916
  97.3 35.5 %copy-start.5 = (f32[1,2,12288]{2,1,0:T(2,128)S(1)}, f32[1,2,12288]{2,1,0:T(2,128)}, u32[]{:S(2)}) copy-start(f32[1,2,12288]{2,1,0:T(2,128)} %param.14) | copy-start | bytes 294916
  97.3 35.5 %copy-start.6 = (f32[1,2,12288]{2,1,0:T(2,128)S(1)}, f32[1,2,12288]{2,1,0:T(2,128)}, u32[]{:S(2)}) copy-start(f32[1,2,12288]{2,1,0:T(2,128)} %param.15) | copy-start | bytes 294916
  134.6 29.3 %all-to-all-start.2 = ((bf16[16,2,12288]{2,1,0:T(2,128)(2,1)}), bf16[16,2,12288]{2,1,0:T(2,128)(2,1)S(1)}, u32[]{:S(2)}, u32[]{:S(2)}) async-start(bf16[16,2,12288]{2,1,0:T(2,128)(2,1)} %broadcast_in_dim.4), calls=%async_computation.2 | async-start | bytes 1572864 | tf_op jit(solution)/shard_map/all_to_all | solution.py:38
where the time goes:
time: 175 us
  waiting for transfers between devices  90.7 us (52%)
  blocking collectives  44.4 us (25%)
  other arithmetic  15.7 us (9%)
  local copies, waits for them, and re-layouts  10.9 us (6%)
  starting transfers between devices  8.79 us (5%)
  matrix products  3.82 us (2%)
    ppermute x1, waiting for transfers between devices, shifted_2(): lax.ppermute(value, axis, [(source, source + steps) for source in range(f...  69.3 us
    all_to_all x1, blocking collectives, summed_rows(): lax.all_to_all(own.astype(jnp.bfloat16), far, 0, 0, tiled=True)  31.5 us
    all_to_all x1, waiting for transfers between devices, from_everyone(): return lax.all_to_all(copies, axis, split_axis=0, concat_axis=0, tiled=True)  21.4 us
    all_to_all x1, starting transfers between devices, from_everyone(): return lax.all_to_all(copies, axis, split_axis=0, concat_axis=0, tiled=True)  6.88 us
    all_to_all x1, blocking collectives, from_everyone(): return lax.all_to_all(copies, axis, split_axis=0, concat_axis=0, tiled=True)  6.7 us
    all_to_all x1, blocking collectives, sent_and_summed(): blocks = lax.all_to_all(split_up(x, dim, devices), axis, 0, 0, tiled=True)  6.15 us
    another operation x2, local copies, waits for them, and re-layouts, split_up(): return jnp.moveaxis(x.reshape(*before, devices, -1, *after), dim, 0)  4.74 us
    dot_general x1, matrix products, term_maker(): lax.dot_general(columns, received, (((0,), (0,)), ((), ())), preferred_el...  3.82 us
  transfers between devices with their start and end apart: 2, of which 2 were waited for; matrix products, arithmetic and copies ran while one was open for 1% of the time, Pallas kernels for 0%

commit v1 on v0

v1 whole, which is shorter than its diff:
```python
import functools

import jax
import jax.numpy as jnp
from jax import lax
from jax.experimental import pallas as pl
from jax.experimental.pallas import tpu as pltpu
from jax.sharding import Mesh
from jax.sharding import PartitionSpec as P

STEP = 20
DP = ("zh", "y", "core")
MESH_ID = pl.DeviceIdType.MESH
F32, BF16 = jnp.float32, jnp.bfloat16
CHUNKS = 4
TILE = 512


def adam_update(grad, master, moment, second):
    new_moment = 0.9 * moment + 0.1 * grad
    new_second = 0.95 * second + 0.05 * grad * grad
    first_fix = 1.0 - 0.9**STEP
    second_fix = 1.0 - 0.95**STEP
    update = new_moment / first_fix / (jnp.sqrt(new_second / second_fix) + 1e-08)
    new_master = master - 0.05 * (update + 0.1 * master)
    return (new_master, new_moment, new_second)


def dot(a, b, dims=((1,), (0,)), precision=None):
    return lax.dot_general(a, b, (dims, ((), ())), preferred_element_type=F32, precision=precision)


def halves(v):
    high = v.astype(BF16)
    return high, (v - high.astype(F32)).astype(BF16)


def kernel(
    n_section,
    x_h, g_h, t_h, gain_h, hid_h, ms_h, mo_h, se_h,
    nms_o, nmo_o, nse_o, w_o,
    tx, gv, gain, hid_own, hid_in, ms, mo, se,
    lhs_tx, lhs_g, lhs_b, cst,
    p_own, p_snd, p_rcv, a_snd, a_rcv, b_snd, b_rcv, z_snd, z_rcv,
    nms, nmo, nse, agz, w8, wall, w_out,
    ld_sem, hid_s, hid_r, d_s, d_r, a_s, a_r, b_s, b_r, z_s, z_r, g_s, g_r, wy_s, wy_r, wd_s, wd_r, o_s,
):
    s = lax.axis_index("section")
    zh, y, core = lax.axis_index("zh"), lax.axis_index("y"), lax.axis_index("core")
    tokens, width = gv.shape
    n_chunk = z_rcv.shape[0]
    span = width // n_chunk
    has_below, has_above, is_last = s > 0, s < n_section - 1, s == n_section - 1
    y_pair, y_far, y_opp = y + 1 - 2 * lax.rem(y, 2), 3 - y, lax.rem(y + 2, 4)
    partner = (s, zh, y, 1 - core)

    def z_at(k):
        return lax.rem(zh + k, 4)

    def roles(c):
        return (y_pair, y_far) if c % 2 == 0 else (y_far, y_pair)

    def cols(c):
        return pl.ds(c * span, span)

    def load(which, c):
        if which == 0:
            return pltpu.make_async_copy(x_h.at[:, cols(c)], tx.at[pl.ds(tokens, tokens), cols(c)], ld_sem.at[0, c])
        if which == 1:
            return pltpu.make_async_copy(g_h.at[:, cols(c)], gv.at[:, cols(c)], ld_sem.at[1, c])
        return pltpu.make_async_copy(t_h.at[:, cols(c)], tx.at[pl.ds(0, tokens), cols(c)], ld_sem.at[2, c])

    small = [
        pltpu.make_async_copy(src, dst, ld_sem.at[3, i])
        for i, (src, dst) in enumerate([(ms_h, ms), (mo_h, mo), (se_h, se)])
    ]
    load_hid = pltpu.make_async_copy(hid_h, hid_own, ld_sem.at[3, 3])
    load_gain = pltpu.make_async_copy(gain_h, gain, ld_sem.at[4, 0])

    load_hid.start()

    @pl.when(is_last)
    def _():
        for c in range(n_chunk):
            load(2, c).start()

    @pl.when(has_below)
    def _():
        for c in range(n_chunk):
            load(0, c).start()
        load_gain.start()
        for c in range(n_chunk):
            load(1, c).start()

    @pl.when(jnp.logical_and(has_below, has_above))
    def _():
        for c in range(n_chunk):
            load(2, c).start()

    for copy in small:
        copy.start()

    barrier = pltpu.get_barrier_semaphore()

    def greet(device):
        pl.semaphore_signal(barrier, inc=1, device_id=device, device_id_type=MESH_ID)

    greet(partner)
    greet((s, zh, y_pair, core))
    greet((s, zh, y_far, core))
    for k in range(1, 4):
        greet((s, z_at(k), y, core))

    @pl.when(has_below)
    def _():
        for k in range(4):
            greet((s - 1, z_at(k), y, core))

    @pl.when(has_above)
    def _():
        for k in range(4):
            greet((s + 1, z_at(k), y, core))

    inner = jnp.logical_and(has_below, has_above)

    @pl.when(inner)
    def _():
        pl.semaphore_wait(barrier, 14)

    @pl.when(jnp.logical_not(inner))
    def _():
        pl.semaphore_wait(barrier, 10)

    def remote(src, dst, send, recv, device):
        return pltpu.make_async_remote_copy(
            src_ref=src, dst_ref=dst, send_sem=send, recv_sem=recv, device_id=device, device_id_type=MESH_ID
        )

    def send_hid():
        return remote(hid_own, hid_in, hid_s, hid_r, (s + 1, zh, y, core))

    load_hid.wait()

    @pl.when(has_above)
    def _():
        send_hid().start()

    def targets(rows):
        other = rows >> 5
        mine = core + other - 2 * core * other
        return ((rows >> 1) & 3) * 16 + ((rows >> 3) & 3) * 4 + mine * 2 + (rows & 1)

    rows = lax.broadcasted_iota(jnp.int32, (64, 64), 0)
    columns = lax.broadcasted_iota(jnp.int32, (64, 64), 1)
    gather_rows = jnp.where(targets(rows) == columns, 1.0, 0.0).astype(F32)
    spread_rows = jnp.where(targets(columns) == rows, 1.0, 0.0).astype(F32).astype(BF16)

    def turned(v):
        return dot(gather_rows.astype(BF16), v).astype(BF16)

    def keep_product(st, c, at, product):
        here = pl.ds(at, TILE)
        p_own[st, c, :, :, here] = product[:32].reshape(4, 8, TILE)
        p_snd[st, c, :, :, here] = product[32:].reshape(4, 8, TILE).astype(BF16)

    def d2d(st, c):
        return remote(p_snd.at[st, c], p_rcv.at[st, c], d_s.at[st, c], d_r.at[st, c], partner)

    def to_a(st, c):
        return remote(a_snd.at[st, c], a_rcv.at[st, c], a_s.at[st, c], a_r.at[st, c], (s, zh, roles(c)[0], core))

    def to_b(st, c):
        return remote(b_snd.at[st, c], b_rcv.at[st, c], b_s.at[st, c], b_r.at[st, c], (s, zh, roles(c)[1], core))

    def to_z(st, c, k):
        section = s - 1 if st == 0 else s
        return remote(
            z_snd.at[st, c, z_at(k)], z_rcv.at[c, zh], z_s.at[st, c, k], z_r.at[c, zh], (section, z_at(k), y, core)
        )

    def from_z(c, k):
        return remote(
            z_snd.at[0, c, z_at(k)], z_rcv.at[c, z_at(k)], z_s.at[0, c, k], z_r.at[c, z_at(k)], (s, z_at(1), y, core)
        )

    def gather_z(c, k):
        return remote(agz.at[c, zh], agz.at[c, zh], g_s.at[c, k - 1], g_r.at[c, zh], (s, z_at(k), y, core))

    def gathered_z(c, k):
        return remote(
            agz.at[c, zh], agz.at[c, z_at(k)], g_s.at[c, k - 1], g_r.at[c, z_at(k)], (s, z_at(k), y, core)
        )

    def along_y(c, which):
        a, b = roles(c)
        block, to = ((y, b), (y, a), (b, a))[which]
        return remote(
            wall.at[c, 0, block], wall.at[c, 0, block], wy_s.at[c, which], wy_r.at[c, which], (s, zh, to, core)
        )

    def arrived_y(c, which):
        a, b = roles(c)
        block = (b, a, y_opp)[which]
        return remote(
            wall.at[c, 0, block], wall.at[c, 0, block], wy_s.at[c, which], wy_r.at[c, which], (s, zh, b, core)
        )

    def over(c, which):
        a, b = roles(c)
        block = (y, b, a, y_opp)[which]
        return remote(
            wall.at[c, 0, block], wall.at[c, 1, block], wd_s.at[c, which], wd_r.at[c, which], partner
        )

    def last_product():
        lhs_b[...] = turned(hid_own[...])
        for c in range(n_chunk):
            load(2, c).wait()

            def step(j, _, c=c):
                at = pl.multiple_of(j * TILE, TILE)
                here = pl.ds(pl.multiple_of(c * span + j * TILE, TILE), TILE)
                keep_product(1, c, at, dot(lhs_b[...], tx[:tokens, here]))
                return 0

            lax.fori_loop(0, span // TILE, step, 0)
            d2d(1, c).start()

    def statistics():
        groups = span // 128
        half = tokens // 2
        sums = jnp.zeros((tokens, 128), F32)
        for c in range(n_chunk):
            load(0, c).wait()

            def step(j, acc, c=c):
                here = pl.ds(pl.multiple_of(c * span + j * 128, 128), 128)
                return acc + tx[tokens:, here].astype(F32)

            sums = lax.fori_loop(0, groups, step, sums)
        mean = jnp.sum(sums, axis=1, keepdims=True) * (1.0 / width)
        load_gain.wait()
        for c in range(n_chunk):
            load(1, c).wait()
        parts = []
        for h in range(2):
            low = h * half
            mean_b = jnp.broadcast_to(mean[low : low + half], (half, 128))
            zero = jnp.zeros((half, 128), F32)

            def step(j, acc, low=low, mean_b=mean_b):
                square, plain, cross = acc
                here = pl.ds(pl.multiple_of(j * 128, 128), 128)
                centred = tx[pl.ds(tokens + low, half), here].astype(F32) - mean_b
                scaled = gv[pl.ds(low, half), here].astype(F32) * gain[:, here]
                return (square + centred * centred, plain + scaled, cross + scaled * centred)

            acc = lax.fori_loop(0, width // 128, step, (zero, zero, zero))
            parts.append([jnp.sum(v, axis=1, keepdims=True) * (1.0 / width) for v in acc])
        var, mean_scaled, cross = (jnp.concatenate([p[i] for p in parts], axis=0) for i in range(3))
        inv = 1.0 / jnp.sqrt(var + 1e-05)
        lane = lax.broadcasted_iota(jnp.int32, (tokens, tokens), 1)
        table = jnp.zeros((tokens, tokens), F32)
        for i, column in enumerate((inv, inv * inv * inv * cross, mean_scaled, mean)):
            table = jnp.where(lane == i, column, table)
        table = table.T
        inv, along, mean_scaled, mean = (table[i : i + 1] for i in range(4))

        send = send_hid()
        send.wait_recv()
        hid = hid_in[...].astype(F32)
        g_high, g_low = halves(hid * inv)
        x_high, x_low = halves(hid * (-along))
        top = turned(hid_in[...])
        lhs_tx[:64, :tokens] = top
        lhs_tx[64:, :tokens] = jnp.zeros_like(top)
        lhs_tx[:64, tokens:] = turned(x_high)
        lhs_tx[64:, tokens:] = turned(x_low)
        lhs_g[:64] = turned(g_high)
        lhs_g[64:] = turned(g_low)
        g_sum = g_high.astype(F32) + g_low.astype(F32)
        x_sum = x_high.astype(F32) + x_low.astype(F32)
        shift = -(g_sum * mean_scaled + x_sum * mean)
        shifted = dot(gather_rows, shift, precision=lax.Precision.HIGHEST)
        cst[...] = jnp.broadcast_to(jnp.sum(shifted, axis=1, keepdims=True), cst.shape)

    def product(c):
        load_c = load(2, c)

        @pl.when(has_above)
        def _():
            load_c.wait()

        def step(j, _):
            at = pl.multiple_of(j * TILE, TILE)
            here = pl.ds(pl.multiple_of(c * span + j * TILE, TILE), TILE)
            plain = dot(lhs_tx[...], tx[:, here])
            scaled = dot(lhs_g[...], gv[:, here])
            whole = plain[:64] + plain[64:] + (scaled[:64] + scaled[64:]) * gain[:, here] + cst[:, :1]
            keep_product(0, c, at, whole)
            return 0

        lax.fori_loop(0, span // TILE, step, 0)
        d2d(0, c).start()

    def pair_sum(st, c):
        a, b = roles(c)
        d2d(st, c).wait_recv()
        for slot, block in enumerate((a, y_opp)):
            a_snd[st, c, slot] = (p_own[st, c, block] + p_rcv[st, c, block].astype(F32)).astype(BF16)
        to_a(st, c).start()

    def first_y(st, c):
        a, b = roles(c)
        to_a(st, c).wait_recv()
        b_snd[st, c] = (
            p_own[st, c, b] + p_rcv[st, c, b].astype(F32) + a_rcv[st, c, 1].astype(F32)
        ).astype(BF16)
        to_b(st, c).start()

    def second_y(st, c):
        to_b(st, c).wait_recv()
        total = (
            p_own[st, c, y] + p_rcv[st, c, y].astype(F32) + a_rcv[st, c, 0].astype(F32) + b_rcv[st, c].astype(F32)
        )
        for q in range(4):
            z_snd[st, c, q] = total[2 * q : 2 * q + 2].astype(BF16)
        if st == 1:
            z_rcv[c, zh] = z_snd[1, c, zh]
        for k in range(st, 4):
            to_z(st, c, k).start()

    def own_rows(c):
        for k in range(1, 4):
            from_z(c, k).wait_recv()

        @pl.when(has_above)
        def _():
            from_z(c, 0).wait_recv()

        grad = sum(z_rcv[c, q].astype(F32) for q in range(4))
        here = cols(c)
        new = adam_update(grad, ms[:, here], mo[:, here], se[:, here])
        nms[:, here], nmo[:, here], nse[:, here] = new
        agz[c, zh] = new[0].astype(BF16)
        for k in range(1, 4):
            gather_z(c, k).start()

    def weights_y(c):
        for k in range(1, 4):
            gathered_z(c, k).wait_recv()
        for q in range(4):
            w8[pl.ds(2 * q, 2), :] = agz[c, q].astype(F32)
        wall[c, 0, y] = w8[...].astype(BF16)
        along_y(c, 0).start()
        along_y(c, 1).start()
        over(c, 0).start()

    def weights_b(c):
        arrived_y(c, 0).wait_recv()
        along_y(c, 2).start()
        over(c, 1).start()

    def weights_a(c):
        arrived_y(c, 1).wait_recv()
        over(c, 2).start()
        arrived_y(c, 2).wait_recv()
        over(c, 3).start()

    def write_weights(c):
        for k in range(4):
            over(c, k).wait_recv()

        def step(j, _):
            at = pl.multiple_of(j * TILE, TILE)
            blocks = wall[c, :, :, :, pl.ds(at, TILE)].astype(F32).reshape(64, TILE).astype(BF16)
            here = pl.ds(pl.multiple_of(c * span + j * TILE, TILE), TILE)
            w_out[:, here] = dot(spread_rows, blocks).astype(BF16)
            return 0

        lax.fori_loop(0, span // TILE, step, 0)
        pltpu.make_async_copy(w_out.at[:, cols(c)], w_o.at[:, cols(c)], o_s.at[c]).start()

    for copy in small:
        copy.wait()

    pl.when(is_last)(last_product)
    pl.when(has_below)(statistics)

    gap = 6.4 / n_chunk
    below, last, always = has_below, is_last, None
    events = []
    for c in range(n_chunk):
        events += [
            (-1.0, c, last, functools.partial(pair_sum, 1, c)),
            (0.5 * gap * c, c, below, functools.partial(product, c)),
            (1.5 + 0.5 * gap * c, c, below, functools.partial(pair_sum, 0, c)),
            (0.8 + gap * c, c, last, functools.partial(first_y, 1, c)),
            (2.8 + gap * c, c, last, functools.partial(second_y, 1, c)),
            (5.0 + gap * c, c, below, functools.partial(first_y, 0, c)),
            (8.0 + gap * c, c, below, functools.partial(second_y, 0, c)),
            (12.5 + gap * c, c, always, functools.partial(own_rows, c)),
            (16.5 + gap * c, c, always, functools.partial(weights_y, c)),
            (19.0 + gap * c, c, always, functools.partial(weights_b, c)),
            (21.5 + gap * c, c, always, functools.partial(weights_a, c)),
            (23.0 + gap * c, c, always, functools.partial(write_weights, c)),
        ]
    for _, _, when, run in sorted(events, key=lambda e: e[:2]):
        if when is None:
            run()
        else:
            pl.when(when)(run)

    states = [
        pltpu.make_async_copy(src, dst, o_s.at[n_chunk + i])
        for i, (src, dst) in enumerate([(nms, nms_o), (nmo, nmo_o), (nse, nse_o)])
    ]
    for copy in states:
        copy.start()

    @pl.when(has_above)
    def _():
        send_hid().wait_send()

    def drain(st):
        for c in range(n_chunk):
            d2d(st, c).wait_send()
            to_a(st, c).wait_send()
            to_b(st, c).wait_send()
            for k in range(st, 4):
                to_z(st, c, k).wait_send()

    pl.when(has_below)(lambda: drain(0))
    pl.when(is_last)(lambda: drain(1))
    for c in range(n_chunk):
        for k in range(1, 4):
            gather_z(c, k).wait_send()
        for k in range(3):
            along_y(c, k).wait_send()
        for k in range(4):
            over(c, k).wait_send()
        pltpu.make_async_copy(w_out.at[:, cols(c)], w_o.at[:, cols(c)], o_s.at[c]).wait()
    for copy in states:
        copy.wait()


def shards(n_section, ln_input, ln_grad, top_grad, ln_gain, hidden, master, moment, second):
    tokens, width = ln_input.shape[1:]
    n_row = hidden.shape[2]
    own = master.shape[1]
    n, span = CHUNKS, width // CHUNKS
    dma = pltpu.SemaphoreType.DMA
    vmem = pltpu.VMEM
    any_space = pl.BlockSpec(memory_space=pl.ANY)
    state = jax.ShapeDtypeStruct((own, width), F32)
    outs = pl.pallas_call(
        functools.partial(kernel, n_section),
        out_shape=(state, state, state, jax.ShapeDtypeStruct((n_row, width), BF16)),
        in_specs=[any_space] * 8,
        out_specs=(any_space,) * 4,
        scratch_shapes=[
            vmem((2 * tokens, width), BF16),
            vmem((tokens, width), BF16),
            vmem((1, width), F32),
            vmem((n_row, tokens), BF16),
            vmem((n_row, tokens), BF16),
            vmem((own, width), F32),
            vmem((own, width), F32),
            vmem((own, width), F32),
            vmem((2 * n_row, 2 * tokens), BF16),
            vmem((2 * n_row, tokens), BF16),
            vmem((n_row, tokens), BF16),
            vmem((n_row, 128), F32),
            vmem((2, n, 4, 8, span), F32),
            vmem((2, n, 4, 8, span), BF16),
            vmem((2, n, 4, 8, span), BF16),
            vmem((2, n, 2, 8, span), BF16),
            vmem((2, n, 2, 8, span), BF16),
            vmem((2, n, 8, span), BF16),
            vmem((2, n, 8, span), BF16),
            vmem((2, n, 4, 2, span), BF16),
            vmem((n, 4, 2, span), BF16),
            vmem((own, width), F32),
            vmem((own, width), F32),
            vmem((own, width), F32),
            vmem((n, 4, 2, span), BF16),
            vmem((8, span), F32),
            vmem((n, 2, 4, 8, span), BF16),
            vmem((n_row, width), BF16),
            dma((5, max(n, 4))),
            dma(()),
            dma(()),
            dma((2, n)),
            dma((2, n)),
            dma((2, n)),
            dma((2, n)),
            dma((2, n)),
            dma((2, n)),
            dma((2, n, 4)),
            dma((n, 4)),
            dma((n, 3)),
            dma((n, 4)),
            dma((n, 3)),
            dma((n, 3)),
            dma((n, 4)),
            dma((n, 4)),
            dma((n + 3,)),
        ],
        compiler_params=pltpu.CompilerParams(
            collective_id=0, has_side_effects=True, vmem_limit_bytes=56 * 1024 * 1024
        ),
    )(ln_input[0], ln_grad[0], top_grad[0], ln_gain, hidden[0].T, master[0], moment[0], second[0])
    return tuple(out[None] for out in outs)


def solution(mesh):
    n_section = mesh.shape["section"]
    finer = Mesh(mesh.devices.reshape(n_section, 4, 4, 2), ("section", *DP))
    rows = P("section", DP, None)
    return jax.shard_map(
        functools.partial(shards, n_section),
        mesh=finer,
        in_specs=(rows, rows, rows, P("section", None), rows, rows, rows, rows),
        out_specs=(rows, rows, rows, P("section", None, None)),
        check_vma=False,
    )
```

time: 175 us -> 71.3 us (0.41)
  the two profiles are of different devices: /device:TPU:3 before, /device:TPU:37 now
where the time goes in v1:
time: 71.3 us; the launch traced here: 71.1 us
  Pallas kernels  63.2 us (89%)
  local copies, waits for them, and re-layouts  7.27 us (10%)
    pallas_call x1, Pallas kernels, shards(): pl.pallas_call(functools.partial(kernel, n_section), out_shape=(state, st...  63.2 us
    unnamed x4, local copies, waits for them, and re-layouts  7.27 us

profile of v1, /device:TPU:37, one launch (start us, length us, event | category | flops | bytes accessed | tf_op | source)
XLA Modules:
  0.0 71.1 jit_solution(12339064746960965503)
XLA Ops:
  0.6 63.2 %shard_map.111 = (f32[2,12288]{1,0:T(2,128)}, f32[2,12288]{1,0:T(2,128)}, f32[2,12288]{1,0:T(2,128)}, bf16[64,12288]{1,0:T(8,128)(2,1)}) custom-call(bf16[128,12288]{1,0:T(8,128)(2,1)} %bitcast.13, bf16[128,12288]{1,0:T(8,128)(2,1)} %bitcast.14, bf16[128,12288]{1,0:T(8,128)(2,1)} %bitcast.15, f32[1,12288]{1,0:T(1,128)} %gain_h.1, bf16[64,128]{1,0:T(8,128)(2,1)} %bitcast.23, ...), custom_call_target="tpu_custom_call" | custom-call | tf_op jit(solution)/shard_map/pallas_call | solution.py:456
  63.9 1.5 %copy.16 = f32[1,2,12288]{2,1,0:T(2,128)} copy(f32[1,2,12288]{2,1,0:T(2,128)} %bitcast.22) | data formatting | bytes 196608
  65.4 1.5 %copy.17 = f32[1,2,12288]{2,1,0:T(2,128)} copy(f32[1,2,12288]{2,1,0:T(2,128)} %bitcast.21) | data formatting | bytes 196608
  66.9 1.5 %copy.18 = f32[1,2,12288]{2,1,0:T(2,128)} copy(f32[1,2,12288]{2,1,0:T(2,128)} %bitcast.20) | data formatting | bytes 196608
  68.5 2.7 %copy.19 = bf16[1,64,12288]{2,1,0:T(8,128)(2,1)} copy(bf16[1,64,12288]{2,1,0:T(8,128)(2,1)} %bitcast.16) | data formatting | bytes 3145728

commit v2 on v1

--- a/solution.py
+++ b/solution.py
@@ -38,12 +38,12 @@
 def kernel(
     n_section,
     x_h, g_h, t_h, gain_h, hid_h, ms_h, mo_h, se_h,
-    nms_o, nmo_o, nse_o, w_o,
+    nms, nmo, nse, w_out,
     tx, gv, gain, hid_own, hid_in, ms, mo, se,
     lhs_tx, lhs_g, lhs_b, cst,
     p_own, p_snd, p_rcv, a_snd, a_rcv, b_snd, b_rcv, z_snd, z_rcv,
-    nms, nmo, nse, agz, w8, wall, w_out,
-    ld_sem, hid_s, hid_r, d_s, d_r, a_s, a_r, b_s, b_r, z_s, z_r, g_s, g_r, wy_s, wy_r, wd_s, wd_r, o_s,
+    agz, w8, wall,
+    ld_sem, hid_s, hid_r, d_s, d_r, a_s, a_r, b_s, b_r, z_s, z_r, g_s, g_r, wy_s, wy_r, wd_s, wd_r,
 ):
     s = lax.axis_index("section")
     zh, y, core = lax.axis_index("zh"), lax.axis_index("y"), lax.axis_index("core")
@@ -121,16 +121,6 @@
         for k in range(4):
             greet((s + 1, z_at(k), y, core))
 
-    inner = jnp.logical_and(has_below, has_above)
-
-    @pl.when(inner)
-    def _():
-        pl.semaphore_wait(barrier, 14)
-
-    @pl.when(jnp.logical_not(inner))
-    def _():
-        pl.semaphore_wait(barrier, 10)
-
     def remote(src, dst, send, recv, device):
         return pltpu.make_async_remote_copy(
             src_ref=src, dst_ref=dst, send_sem=send, recv_sem=recv, device_id=device, device_id_type=MESH_ID
@@ -139,11 +129,29 @@
     def send_hid():
         return remote(hid_own, hid_in, hid_s, hid_r, (s + 1, zh, y, core))
 
-    load_hid.wait()
-
-    @pl.when(has_above)
-    def _():
-        send_hid().start()
+    def ready():
+        inner = jnp.logical_and(has_below, has_above)
+
+        @pl.when(has_above)
+        def _():
+            load_hid.wait()
+
+        @pl.when(inner)
+        def _():
+            pl.semaphore_wait(barrier, 14)
+
+        @pl.when(jnp.logical_not(inner))
+        def _():
+            pl.semaphore_wait(barrier, 10)
+
+        @pl.when(has_above)
+        def _():
+            send_hid().start()
+
+        @pl.when(is_last)
+        def _():
+            for c in range(n_chunk):
+                d2d(1, c).start()
 
     def targets(rows):
         other = rows >> 5
@@ -213,6 +221,7 @@
         )
 
     def last_product():
+        load_hid.wait()
         lhs_b[...] = turned(hid_own[...])
         for c in range(n_chunk):
             load(2, c).wait()
@@ -223,12 +232,10 @@
                 keep_product(1, c, at, dot(lhs_b[...], tx[:tokens, here]))
                 return 0
 
-            lax.fori_loop(0, span // TILE, step, 0)
-            d2d(1, c).start()
+            lax.fori_loop(0, span // TILE, step, 0, unroll=2)
 
     def statistics():
         groups = span // 128
-        half = tokens // 2
         sums = jnp.zeros((tokens, 128), F32)
         for c in range(n_chunk):
             load(0, c).wait()
@@ -237,26 +244,29 @@
                 here = pl.ds(pl.multiple_of(c * span + j * 128, 128), 128)
                 return acc + tx[tokens:, here].astype(F32)
 
-            sums = lax.fori_loop(0, groups, step, sums)
+            sums = lax.fori_loop(0, groups, step, sums, unroll=4)
         mean = jnp.sum(sums, axis=1, keepdims=True) * (1.0 / width)
         load_gain.wait()
         for c in range(n_chunk):
             load(1, c).wait()
         parts = []
-        for h in range(2):
-            low = h * half
-            mean_b = jnp.broadcast_to(mean[low : low + half], (half, 128))
-            zero = jnp.zeros((half, 128), F32)
+        part = 32
+        for low in range(0, tokens, part):
+            mean_b = jnp.broadcast_to(mean[low : low + part], (part, 128))
+            zero = jnp.zeros((part, 128), F32)
 
             def step(j, acc, low=low, mean_b=mean_b):
                 square, plain, cross = acc
                 here = pl.ds(pl.multiple_of(j * 128, 128), 128)
-                centred = tx[pl.ds(tokens + low, half), here].astype(F32) - mean_b
-                scaled = gv[pl.ds(low, half), here].astype(F32) * gain[:, here]
+                centred = tx[pl.ds(tokens + low, part), here].astype(F32) - mean_b
+                scaled = gv[pl.ds(low, part), here].astype(F32) * gain[:, here]
                 return (square + centred * centred, plain + scaled, cross + scaled * centred)
 
-            acc = lax.fori_loop(0, width // 128, step, (zero, zero, zero))
+            acc = lax.fori_loop(0, width // 128, step, (zero, zero, zero), unroll=8)
             parts.append([jnp.sum(v, axis=1, keepdims=True) * (1.0 / width) for v in acc])
+            if low == 2 * part:
+                with jax.named_scope("ready"):
+                    ready()
         var, mean_scaled, cross = (jnp.concatenate([p[i] for p in parts], axis=0) for i in range(3))
         inv = 1.0 / jnp.sqrt(var + 1e-05)
         lane = lax.broadcasted_iota(jnp.int32, (tokens, tokens), 1)
@@ -266,8 +276,8 @@
         table = table.T
         inv, along, mean_scaled, mean = (table[i : i + 1] for i in range(4))
 
-        send = send_hid()
-        send.wait_recv()
+        with jax.named_scope("hid_wait"):
+            send_hid().wait_recv()
         hid = hid_in[...].astype(F32)
         g_high, g_low = halves(hid * inv)
         x_high, x_low = halves(hid * (-along))
@@ -300,7 +310,7 @@
             keep_product(0, c, at, whole)
             return 0
 
-        lax.fori_loop(0, span // TILE, step, 0)
+        lax.fori_loop(0, span // TILE, step, 0, unroll=2)
         d2d(0, c).start()
 
     def pair_sum(st, c):
@@ -331,6 +341,9 @@
             to_z(st, c, k).start()
 
     def own_rows(c):
+        if c == 0:
+            for copy in small:
+                copy.wait()
         for k in range(1, 4):
             from_z(c, k).wait_recv()
 
@@ -378,14 +391,14 @@
             w_out[:, here] = dot(spread_rows, blocks).astype(BF16)
             return 0
 
-        lax.fori_loop(0, span // TILE, step, 0)
-        pltpu.make_async_copy(w_out.at[:, cols(c)], w_o.at[:, cols(c)], o_s.at[c]).start()
-
-    for copy in small:
-        copy.wait()
-
-    pl.when(is_last)(last_product)
-    pl.when(has_below)(statistics)
+        lax.fori_loop(0, span // TILE, step, 0, unroll=2)
+
+    with jax.named_scope("last_product"):
+        pl.when(is_last)(last_product)
+    with jax.named_scope("ready_0"):
+        pl.when(jnp.logical_not(has_below))(ready)
+    with jax.named_scope("statistics"):
+        pl.when(has_below)(statistics)
 
     gap = 6.4 / n_chunk
     below, last, always = has_below, is_last, None
@@ -405,18 +418,12 @@
             (21.5 + gap * c, c, always, functools.partial(weights_a, c)),
             (23.0 + gap * c, c, always, functools.partial(write_weights, c)),
         ]
-    for _, _, when, run in sorted(events, key=lambda e: e[:2]):
-        if when is None:
-            run()
-        else:
-            pl.when(when)(run)
-
-    states = [
-        pltpu.make_async_copy(src, dst, o_s.at[n_chunk + i])
-        for i, (src, dst) in enumerate([(nms, nms_o), (nmo, nmo_o), (nse, nse_o)])
-    ]
-    for copy in states:
-        copy.start()
+    for _, c, when, run in sorted(events, key=lambda e: e[:2]):
+        with jax.named_scope(f"{run.func.__name__}_{c}"):
+            if when is None:
+                run()
+            else:
+                pl.when(when)(run)
 
     @pl.when(has_above)
     def _():
@@ -439,8 +446,14 @@
             along_y(c, k).wait_send()
         for k in range(4):
             over(c, k).wait_send()
-        pltpu.make_async_copy(w_out.at[:, cols(c)], w_o.at[:, cols(c)], o_s.at[c]).wait()
-    for copy in states:
+
+
+def store(*refs):
+    *refs, sems = refs
+    copies = [pltpu.make_async_copy(refs[i], refs[4 + i], sems.at[i]) for i in range(4)]
+    for copy in copies:
+        copy.start()
+    for copy in copies:
         copy.wait()
 
 
@@ -452,12 +465,12 @@
     dma = pltpu.SemaphoreType.DMA
     vmem = pltpu.VMEM
     any_space = pl.BlockSpec(memory_space=pl.ANY)
-    state = jax.ShapeDtypeStruct((own, width), F32)
+    results = (((own, width), F32),) * 3 + (((n_row, width), BF16),)
     outs = pl.pallas_call(
         functools.partial(kernel, n_section),
-        out_shape=(state, state, state, jax.ShapeDtypeStruct((n_row, width), BF16)),
+        out_shape=tuple(vmem(*r) for r in results),
         in_specs=[any_space] * 8,
-        out_specs=(any_space,) * 4,
+        out_specs=(pl.BlockSpec(memory_space=vmem),) * 4,
         scratch_shapes=[
             vmem((2 * tokens, width), BF16),
             vmem((tokens, width), BF16),
@@ -480,13 +493,9 @@
             vmem((2, n, 8, span), BF16),
             vmem((2, n, 4, 2, span), BF16),
             vmem((n, 4, 2, span), BF16),
-            vmem((own, width), F32),
-            vmem((own, width), F32),
-            vmem((own, width), F32),
             vmem((n, 4, 2, span), BF16),
             vmem((8, span), F32),
             vmem((n, 2, 4, 8, span), BF16),
-            vmem((n_row, width), BF16),
             dma((5, max(n, 4))),
             dma(()),
             dma(()),
@@ -504,12 +513,18 @@
             dma((n, 3)),
             dma((n, 4)),
             dma((n, 4)),
-            dma((n + 3,)),
         ],
         compiler_params=pltpu.CompilerParams(
             collective_id=0, has_side_effects=True, vmem_limit_bytes=56 * 1024 * 1024
         ),
     )(ln_input[0], ln_grad[0], top_grad[0], ln_gain, hidden[0].T, master[0], moment[0], second[0])
+    outs = pl.pallas_call(
+        store,
+        out_shape=tuple(jax.ShapeDtypeStruct(*r) for r in results),
+        in_specs=[pl.BlockSpec(memory_space=vmem)] * 4,
+        out_specs=(any_space,) * 4,
+        scratch_shapes=[dma((4,))],
+    )(*(pltpu.with_memory_space_constraint(out, vmem) for out in outs))
     return tuple(out[None] for out in outs)
 
 

time: 71.3 us -> 57.3 us (0.80)
  local copies, waits for them, and re-layouts: 7.27 us -> 0 us
  Pallas kernels: 63.2 us -> 56.5 us
    unnamed x4 -> x0, local copies, waits for them, and re-layouts: 7.27 us -> none
    pallas_call x1 -> x2, Pallas kernels: 63.2 us -> 56.5 us  [the longest x1 55.2 us: shards(): pl.pallas_call(functools.partial(kernel, n_section), out_shape=tuple((vme...]
where the time goes in v2:
time: 57.3 us; the launch traced here: 57.1 us
  Pallas kernels  56.5 us (99%)
  between operations  0.64 us (1%)
    pallas_call x1, Pallas kernels, shards(): pl.pallas_call(functools.partial(kernel, n_section), out_shape=tuple((vme...  55.2 us
    pallas_call x1, Pallas kernels, shards(): pl.pallas_call(store, out_shape=tuple((jax.ShapeDtypeStruct(*r) for r in...  1.28 us

profile of v2, /device:TPU:37, one launch (start us, length us, event | category | flops | bytes accessed | tf_op | source)
XLA Modules:
  0.0 57.1 jit_solution(9879322706338672682)
XLA Ops:
  0.6 55.2 %shard_map.111 = (f32[2,12288]{1,0:T(2,128)S(1)}, f32[2,12288]{1,0:T(2,128)S(1)}, f32[2,12288]{1,0:T(2,128)S(1)}, bf16[64,12288]{1,0:T(8,128)(2,1)S(1)}) custom-call(bf16[128,12288]{1,0:T(8,128)(2,1)} %bitcast.13, bf16[128,12288]{1,0:T(8,128)(2,1)} %bitcast.14, bf16[128,12288]{1,0:T(8,128)(2,1)} %bitcast.15, f32[1,12288]{1,0:T(1,128)} %gain_h.1, ...), custom_call_target="tpu_custom_call" | custom-call | tf_op jit(solution)/shard_map/pallas_call | solution.py:469
  55.8 1.3 %shard_map.112 = (f32[2,12288]{1,0:T(2,128)}, f32[2,12288]{1,0:T(2,128)}, f32[2,12288]{1,0:T(2,128)}, bf16[64,12288]{1,0:T(8,128)(2,1)}) custom-call(f32[2,12288]{1,0:T(2,128)S(1)} %get-tuple-element.12.refs_0_, f32[2,12288]{1,0:T(2,128)S(1)} %get-tuple-element.13.refs_1_, f32[2,12288]{1,0:T(2,128)S(1)} %get-tuple-element.14.refs_2_, ...), custom_call_target="tpu_custom_call" | custom-call | tf_op jit(solution)/shard_map/pallas_call | solution.py:521

commit v3 on v2

--- a/solution.py
+++ b/solution.py
@@ -12,7 +12,7 @@
 DP = ("zh", "y", "core")
 MESH_ID = pl.DeviceIdType.MESH
 F32, BF16 = jnp.float32, jnp.bfloat16
-CHUNKS = 4
+CHUNKS = 8
 TILE = 512
 
 
@@ -51,14 +51,21 @@
     n_chunk = z_rcv.shape[0]
     span = width // n_chunk
     has_below, has_above, is_last = s > 0, s < n_section - 1, s == n_section - 1
-    y_pair, y_far, y_opp = y + 1 - 2 * lax.rem(y, 2), 3 - y, lax.rem(y + 2, 4)
+    mine = (y, zh)
+    pair_of, far_of, opp_of = ([f(i) for i in mine] for f in (lambda i: i + 1 - 2 * lax.rem(i, 2), lambda i: 3 - i, lambda i: lax.rem(i + 2, 4)))
     partner = (s, zh, y, 1 - core)
 
     def z_at(k):
         return lax.rem(zh + k, 4)
 
-    def roles(c):
-        return (y_pair, y_far) if c % 2 == 0 else (y_far, y_pair)
+    def y_at(k):
+        return lax.rem(y + k, 4)
+
+    def roles(st, c):
+        return (pair_of[st], far_of[st]) if c % 2 == 0 else (far_of[st], pair_of[st])
+
+    def at(st, index):
+        return (s, zh, index, core) if st == 0 else (s, index, y, core)
 
     def cols(c):
         return pl.ds(c * span, span)
@@ -106,10 +113,14 @@
         pl.semaphore_signal(barrier, inc=1, device_id=device, device_id_type=MESH_ID)
 
     greet(partner)
-    greet((s, zh, y_pair, core))
-    greet((s, zh, y_far, core))
+    greet((s, zh, pair_of[0], core))
+    greet((s, zh, far_of[0], core))
     for k in range(1, 4):
         greet((s, z_at(k), y, core))
+
+    @pl.when(is_last)
+    def _():
+        greet((s, zh, opp_of[0], core))
 
     @pl.when(has_below)
     def _():
@@ -140,9 +151,13 @@
         def _():
             pl.semaphore_wait(barrier, 14)
 
-        @pl.when(jnp.logical_not(inner))
+        @pl.when(jnp.logical_not(has_below))
         def _():
             pl.semaphore_wait(barrier, 10)
+
+        @pl.when(is_last)
+        def _():
+            pl.semaphore_wait(barrier, 11)
 
         @pl.when(has_above)
         def _():
@@ -153,18 +168,18 @@
             for c in range(n_chunk):
                 d2d(1, c).start()
 
-    def targets(rows):
+    def targets(rows, y_shift=3, z_shift=1):
         other = rows >> 5
-        mine = core + other - 2 * core * other
-        return ((rows >> 1) & 3) * 16 + ((rows >> 3) & 3) * 4 + mine * 2 + (rows & 1)
+        whose = core + other - 2 * core * other
+        return ((rows >> z_shift) & 3) * 16 + ((rows >> y_shift) & 3) * 4 + whose * 2 + (rows & 1)
 
     rows = lax.broadcasted_iota(jnp.int32, (64, 64), 0)
     columns = lax.broadcasted_iota(jnp.int32, (64, 64), 1)
     gather_rows = jnp.where(targets(rows) == columns, 1.0, 0.0).astype(F32)
     spread_rows = jnp.where(targets(columns) == rows, 1.0, 0.0).astype(F32).astype(BF16)
 
-    def turned(v):
-        return dot(gather_rows.astype(BF16), v).astype(BF16)
+    def turned(v, order=gather_rows):
+        return dot(order.astype(BF16), v).astype(BF16)
 
     def keep_product(st, c, at, product):
         here = pl.ds(at, TILE)
@@ -175,21 +190,24 @@
         return remote(p_snd.at[st, c], p_rcv.at[st, c], d_s.at[st, c], d_r.at[st, c], partner)
 
     def to_a(st, c):
-        return remote(a_snd.at[st, c], a_rcv.at[st, c], a_s.at[st, c], a_r.at[st, c], (s, zh, roles(c)[0], core))
+        return remote(a_snd.at[st, c], a_rcv.at[st, c], a_s.at[st, c], a_r.at[st, c], at(st, roles(st, c)[0]))
 
     def to_b(st, c):
-        return remote(b_snd.at[st, c], b_rcv.at[st, c], b_s.at[st, c], b_r.at[st, c], (s, zh, roles(c)[1], core))
-
-    def to_z(st, c, k):
-        section = s - 1 if st == 0 else s
+        return remote(b_snd.at[st, c], b_rcv.at[st, c], b_s.at[st, c], b_r.at[st, c], at(st, roles(st, c)[1]))
+
+    def to_owner(st, c, k):
+        slot = z_at(k) if st == 0 else y_at(k)
         return remote(
-            z_snd.at[st, c, z_at(k)], z_rcv.at[c, zh], z_s.at[st, c, k], z_r.at[c, zh], (section, z_at(k), y, core)
-        )
-
-    def from_z(c, k):
-        return remote(
-            z_snd.at[0, c, z_at(k)], z_rcv.at[c, z_at(k)], z_s.at[0, c, k], z_r.at[c, z_at(k)], (s, z_at(1), y, core)
-        )
+            z_snd.at[st, c, slot],
+            z_rcv.at[c, mine[1 - st]],
+            z_s.at[st, c, k],
+            z_r.at[c, mine[1 - st]],
+            (s - 1, slot, y, core) if st == 0 else (s, zh, slot, core),
+        )
+
+    def to_own(st, c, k):
+        slot = z_at(k) if st == 0 else y_at(k)
+        return remote(z_snd.at[st, c, slot], z_rcv.at[c, slot], z_s.at[st, c, k], z_r.at[c, slot], partner)
 
     def gather_z(c, k):
         return remote(agz.at[c, zh], agz.at[c, zh], g_s.at[c, k - 1], g_r.at[c, zh], (s, z_at(k), y, core))
@@ -200,29 +218,29 @@
         )
 
     def along_y(c, which):
-        a, b = roles(c)
+        a, b = roles(0, c)
         block, to = ((y, b), (y, a), (b, a))[which]
         return remote(
             wall.at[c, 0, block], wall.at[c, 0, block], wy_s.at[c, which], wy_r.at[c, which], (s, zh, to, core)
         )
 
     def arrived_y(c, which):
-        a, b = roles(c)
-        block = (b, a, y_opp)[which]
+        a, b = roles(0, c)
+        block = (b, a, opp_of[0])[which]
         return remote(
             wall.at[c, 0, block], wall.at[c, 0, block], wy_s.at[c, which], wy_r.at[c, which], (s, zh, b, core)
         )
 
     def over(c, which):
-        a, b = roles(c)
-        block = (y, b, a, y_opp)[which]
+        a, b = roles(0, c)
+        block = (y, b, a, opp_of[0])[which]
         return remote(
             wall.at[c, 0, block], wall.at[c, 1, block], wd_s.at[c, which], wd_r.at[c, which], partner
         )
 
     def last_product():
         load_hid.wait()
-        lhs_b[...] = turned(hid_own[...])
+        lhs_b[...] = turned(hid_own[...], jnp.where(targets(rows, 1, 3) == columns, 1.0, 0.0))
         for c in range(n_chunk):
             load(2, c).wait()
 
@@ -275,6 +293,13 @@
             table = jnp.where(lane == i, column, table)
         table = table.T
         inv, along, mean_scaled, mean = (table[i : i + 1] for i in range(4))
+
+        with jax.named_scope("pair_b"):
+
+            @pl.when(is_last)
+            def _():
+                for c in range(n_chunk):
+                    pair_sum(1, c)
 
         with jax.named_scope("hid_wait"):
             send_hid().wait_recv()
@@ -314,14 +339,14 @@
         d2d(0, c).start()
 
     def pair_sum(st, c):
-        a, b = roles(c)
+        a = roles(st, c)[0]
         d2d(st, c).wait_recv()
-        for slot, block in enumerate((a, y_opp)):
+        for slot, block in enumerate((a, opp_of[st])):
             a_snd[st, c, slot] = (p_own[st, c, block] + p_rcv[st, c, block].astype(F32)).astype(BF16)
         to_a(st, c).start()
 
     def first_y(st, c):
-        a, b = roles(c)
+        b = roles(st, c)[1]
         to_a(st, c).wait_recv()
         b_snd[st, c] = (
             p_own[st, c, b] + p_rcv[st, c, b].astype(F32) + a_rcv[st, c, 1].astype(F32)
@@ -331,25 +356,32 @@
     def second_y(st, c):
         to_b(st, c).wait_recv()
         total = (
-            p_own[st, c, y] + p_rcv[st, c, y].astype(F32) + a_rcv[st, c, 0].astype(F32) + b_rcv[st, c].astype(F32)
+            p_own[st, c, mine[st]]
+            + p_rcv[st, c, mine[st]].astype(F32)
+            + a_rcv[st, c, 0].astype(F32)
+            + b_rcv[st, c].astype(F32)
         )
         for q in range(4):
             z_snd[st, c, q] = total[2 * q : 2 * q + 2].astype(BF16)
         if st == 1:
-            z_rcv[c, zh] = z_snd[1, c, zh]
+            z_rcv[c, y] = z_snd[1, c, y]
         for k in range(st, 4):
-            to_z(st, c, k).start()
+            to_owner(st, c, k).start()
 
     def own_rows(c):
         if c == 0:
             for copy in small:
                 copy.wait()
-        for k in range(1, 4):
-            from_z(c, k).wait_recv()
 
         @pl.when(has_above)
         def _():
-            from_z(c, 0).wait_recv()
+            for k in range(4):
+                to_own(0, c, k).wait_recv()
+
+        @pl.when(is_last)
+        def _():
+            for k in range(1, 4):
+                to_own(1, c, k).wait_recv()
 
         grad = sum(z_rcv[c, q].astype(F32) for q in range(4))
         here = cols(c)
@@ -400,23 +432,22 @@
     with jax.named_scope("statistics"):
         pl.when(has_below)(statistics)
 
-    gap = 6.4 / n_chunk
     below, last, always = has_below, is_last, None
     events = []
     for c in range(n_chunk):
+        part = c / n_chunk
         events += [
-            (-1.0, c, last, functools.partial(pair_sum, 1, c)),
-            (0.5 * gap * c, c, below, functools.partial(product, c)),
-            (1.5 + 0.5 * gap * c, c, below, functools.partial(pair_sum, 0, c)),
-            (0.8 + gap * c, c, last, functools.partial(first_y, 1, c)),
-            (2.8 + gap * c, c, last, functools.partial(second_y, 1, c)),
-            (5.0 + gap * c, c, below, functools.partial(first_y, 0, c)),
-            (8.0 + gap * c, c, below, functools.partial(second_y, 0, c)),
-            (12.5 + gap * c, c, always, functools.partial(own_rows, c)),
-            (16.5 + gap * c, c, always, functools.partial(weights_y, c)),
-            (19.0 + gap * c, c, always, functools.partial(weights_b, c)),
-            (21.5 + gap * c, c, always, functools.partial(weights_a, c)),
-            (23.0 + gap * c, c, always, functools.partial(write_weights, c)),
+            (0 + part, c, below, functools.partial(product, c)),
+            (0.4 + part, c, below, functools.partial(pair_sum, 0, c)),
+            (2 + part, c, last, functools.partial(first_y, 1, c)),
+            (3 + part, c, below, functools.partial(first_y, 0, c)),
+            (4 + part, c, last, functools.partial(second_y, 1, c)),
+            (5 + part, c, below, functools.partial(second_y, 0, c)),
+            (6 + part, c, always, functools.partial(own_rows, c)),
+            (7 + part, c, always, functools.partial(weights_y, c)),
+            (8 + part, c, always, functools.partial(weights_b, c)),
+            (9 + part, c, always, functools.partial(weights_a, c)),
+            (9.4 + part, c, always, functools.partial(write_weights, c)),
         ]
     for _, c, when, run in sorted(events, key=lambda e: e[:2]):
         with jax.named_scope(f"{run.func.__name__}_{c}"):
@@ -435,7 +466,7 @@
             to_a(st, c).wait_send()
             to_b(st, c).wait_send()
             for k in range(st, 4):
-                to_z(st, c, k).wait_send()
+                to_owner(st, c, k).wait_send()
 
     pl.when(has_below)(lambda: drain(0))
     pl.when(is_last)(lambda: drain(1))

time: 57.3 us -> 52.5 us (0.916)
  the two profiles are of different devices: /device:TPU:37 before, /device:TPU:7 now
where the time goes in v3:
time: 52.5 us; the launch traced here: 52.3 us
  Pallas kernels  51.7 us (98%)
  between operations  0.64 us (1%)
    pallas_call x1, Pallas kernels, shards(): pl.pallas_call(functools.partial(kernel, n_section), out_shape=tuple((vme...  50.4 us
    pallas_call x1, Pallas kernels, shards(): pl.pallas_call(store, out_shape=tuple((jax.ShapeDtypeStruct(*r) for r in...  1.28 us

profile of v3, /device:TPU:7, one launch (start us, length us, event | category | flops | bytes accessed | tf_op | source)
XLA Modules:
  0.0 52.3 jit_solution(18342677465651934946)
XLA Ops:
  0.6 50.4 %shard_map.111 = (f32[2,12288]{1,0:T(2,128)S(1)}, f32[2,12288]{1,0:T(2,128)S(1)}, f32[2,12288]{1,0:T(2,128)S(1)}, bf16[64,12288]{1,0:T(8,128)(2,1)S(1)}) custom-call(bf16[128,12288]{1,0:T(8,128)(2,1)} %bitcast.13, bf16[128,12288]{1,0:T(8,128)(2,1)} %bitcast.14, bf16[128,12288]{1,0:T(8,128)(2,1)} %bitcast.15, f32[1,12288]{1,0:T(1,128)} %gain_h.1, ...), custom_call_target="tpu_custom_call" | custom-call | tf_op jit(solution)/shard_map/pallas_call | solution.py:500
  51.1 1.3 %shard_map.112 = (f32[2,12288]{1,0:T(2,128)}, f32[2,12288]{1,0:T(2,128)}, f32[2,12288]{1,0:T(2,128)}, bf16[64,12288]{1,0:T(8,128)(2,1)}) custom-call(f32[2,12288]{1,0:T(2,128)S(1)} %get-tuple-element.12.refs_0_, f32[2,12288]{1,0:T(2,128)S(1)} %get-tuple-element.13.refs_1_, f32[2,12288]{1,0:T(2,128)S(1)} %get-tuple-element.14.refs_2_, ...), custom_call_target="tpu_custom_call" | custom-call | tf_op jit(solution)/shard_map/pallas_call | solution.py:552
